TPU v7x, 128 devices: a whole 4x4x4 slice. The times are simulated.
128 devices in a mesh: dp: 8 (over x, y_hi), expert: 16 (over z, y_lo, core).
Axes of the slice: x: 4, y: 4 (y_hi: 2, y_lo: 2; y = y_hi * 2 + y_lo), z: 4, core: 2. Of those that a mesh axis runs over, the one named last changes fastest.
Arguments:
- tokens: bfloat16 [16384, 4096], P(('dp', 'expert')), may hold values from -6 to 6
- cotangent: bfloat16 [16384, 4096], P(('dp', 'expert')), may hold values from -3 to 3
- expert_ids: int32 [16384, 8, 2], P(('dp', 'expert')), may hold values from 0 to 31, as said below
- slot_ids: int32 [16384, 8, 2], P(('dp', 'expert')), may hold values from 0 to 63, as said below
- route_probs: bfloat16 [16384, 8, 2], P(('dp', 'expert')), may hold values from 0.099609375 to 1
- weights_in: bfloat16 [32, 2, 1792, 512], P('expert', None, 'dp'), may hold values from -0.25 to 0.25
- weights_out: bfloat16 [32, 1792, 512], P('expert', 'dp'), may hold values from -0.125 to 0.125
Outputs:
- grad_tokens: bfloat16 [16384, 4096], P(('dp', 'expert'))
- grad_probs: float32 [16384, 8, 2], P(('dp', 'expert'))
- grad_in: bfloat16 [32, 2, 1792, 512], P('expert', None, 'dp')
- grad_out: bfloat16 [32, 1792, 512], P('expert', 'dp')
Inputs may be any that keep to these rules, and one draw needn't show every extreme that they name: `expert_ids`: each sub-token names 2 different experts. On each device the experts fall into two sets of 16, and the two ids of a sub-token come one from each set. Every expert is named by exactly 64 sub-tokens of every device. `slot_ids`: for each device and expert, the sub-tokens of that device that name the expert carry distinct slot numbers at the matching position.
All inputs are finite; a program needn't handle non-finite values.
Results may differ from a plain program's by a relative error of at most 0.012.
Values may be sent and summed in bfloat16 or wider, within the bound.
No kernel may reach another device: no remote copies, remote signals or barrier semaphores. Data moves between devices by JAX's collectives and lax.ppermute only.
A program may use at most 192 MiB of HBM per device.

v0:
```python
import functools

import jax
import jax.numpy as jnp
from jax import lax
from jax.experimental import pallas as pl
from jax.experimental.pallas import tpu as pltpu
from jax.sharding import Mesh
from jax.sharding import PartitionSpec as P

H = 8
DS = 512
PEERS = 32
SLOTS = (40, 24)
GROUP = 8
SUBS = 1024
EXTRA = 8
SH = 224
F32 = jnp.float32
BF = jnp.bfloat16
AXES = ("x", "yh", "z", "yl", "core")
PLANE = ("yh", "z", "yl", "core")


def contract(a, b, ca, cb):
    return lax.dot_general(a, b, (((ca,), (cb,)), ((), ())), preferred_element_type=F32)


def in_hbm(a):
    return pltpu.with_memory_space_constraint(a, pltpu.HBM)


def params(mib=24):
    return pltpu.CompilerParams(vmem_limit_bytes=mib * 2**20)


def dispatch_kernel(table, tok, cot, out, *, part):
    slots = SLOTS[part]
    base = part * PEERS * SLOTS[0]
    x = jnp.concatenate([tok[:, h * DS : (h + 1) * DS] for h in range(H)], axis=0)
    c = jnp.concatenate([cot[:, h * DS : (h + 1) * DS] for h in range(H)], axis=0)
    code0 = table[0:1, :].astype(jnp.int32)
    code1 = table[1:2, :].astype(jnp.int32)
    prob0 = table[2:3, :]
    prob1 = table[3:4, :]
    block = GROUP * slots
    row = lax.broadcasted_iota(jnp.int32, (block, SUBS), 0) + (base + pl.program_id(0) * block)
    hit0 = row == code0
    hit1 = row == code1
    scale = jnp.where(hit0, prob0, jnp.where(hit1, prob1, 0.0)).astype(BF)
    pick = jnp.where(hit0 | hit1, 1.0, 0.0).astype(BF)
    out[:, 0:slots, :] = contract(pick, x, 1, 0).astype(BF).reshape(GROUP, slots, DS)
    out[:, slots : 2 * slots, :] = contract(scale, c, 1, 0).astype(BF).reshape(GROUP, slots, DS)


def dispatch(table, tok, cot, part):
    slots = SLOTS[part]
    fixed = lambda b: (0, 0)
    return pl.pallas_call(
        functools.partial(dispatch_kernel, part=part),
        grid=(PEERS // GROUP,),
        in_specs=[
            pl.BlockSpec((8, SUBS), fixed),
            pl.BlockSpec((SUBS // H, H * DS), fixed),
            pl.BlockSpec((SUBS // H, H * DS), fixed),
        ],
        out_specs=pl.BlockSpec((GROUP, 2 * slots, DS), lambda b: (b, 0, 0)),
        out_shape=pltpu.HBM((PEERS, 2 * slots, DS), BF),
        compiler_params=params(),
    )(table, tok, cot)


def expert_block(z, slots, wg, wu, wo):
    hidden = wg.shape[0]
    rows = PEERS * slots
    x = z[:, 0:slots, :].reshape(rows, DS)
    s = z[:, slots : 2 * slots, :].reshape(rows, DS)
    g = contract(wg, x, 1, 1)
    u = contract(wu, x, 1, 1)
    dh = contract(wo, s, 1, 1)
    sig = 0.5 * jnp.tanh(0.5 * g) + 0.5
    act = g * sig
    hid = (act * u).astype(BF)
    dhu = dh * u
    du = (dh * act).astype(BF)
    dg = (dhu * (sig + act * (1.0 - sig))).astype(BF)
    router = jnp.sum((dhu * act).reshape(hidden // 8, 8, rows), axis=0)
    dw = (contract(dg, x, 1, 0), contract(du, x, 1, 0), contract(hid, s, 1, 0))
    dx = contract(dg, wg, 0, 0) + contract(du, wu, 0, 0)
    return dw, dx, router


HBM = pl.BlockSpec(memory_space=pltpu.HBM)
WHOLE = pl.BlockSpec(memory_space=pltpu.VMEM)
UNITS = 2 * SH


def router_rows(back, at, router_first, router):
    table = jnp.zeros((PEERS, 128), F32)
    for part, value in ((0, router_first), (1, router)):
        count = SLOTS[part]
        total = PEERS * count
        source = lax.broadcasted_iota(jnp.int32, (PEERS, total), 0) * count
        row = lax.broadcasted_iota(jnp.int32, (PEERS, total), 1)
        flat = jnp.sum(value, axis=0, keepdims=True)
        spread = jnp.where((row >= source) & (row < source + count), flat, 0.0).astype(BF)
        slot = lax.broadcasted_iota(jnp.int32, (total, 128), 0) % count + part * SLOTS[0]
        lane = lax.broadcasted_iota(jnp.int32, (total, 128), 1)
        place = jnp.where(slot == lane, 1.0, 0.0).astype(BF)
        table = table + contract(spread, place, 1, 0)
    back[:, :, at : at + 128] = jnp.broadcast_to(table.astype(BF)[:, None, :], (PEERS, EXTRA, 128))


def expert_kernel(*refs, part, pairs, first, begin, end):
    slots = SLOTS[part]
    last = part == 1 and end
    refs = list(refs)
    take = lambda n: [refs.pop(0) for _ in range(n)]
    (z_in,) = take(1)
    weights = take(2 * pairs)
    before = take(1)[0] if part else None
    acc_in, router_in = (None, None) if begin else take(2)
    router_first = take(1)[0] if last else None
    outs = take(2 * pairs if part else 1)
    (dx_out,) = take(1)
    router_out = None if last else take(1)[0]
    z, acc, wbuf, stage, obuf, dbuf, zsem, asem, wsem, bsem, ssem = refs

    def units(p):
        return pl.ds(pl.multiple_of(p * UNITS, UNITS), UNITS)

    def fetch(k, slot):
        half = k % 2
        return pltpu.make_async_copy(
            weights[k], wbuf.at[slot, :, half * SH : (half + 1) * SH, :], wsem.at[slot, half]
        )

    def load(p):
        return pltpu.make_async_copy(before.at[:, units(first + p), :], stage.at[p], bsem.at[p])

    def store_wide(p):
        return pltpu.make_async_copy(stage.at[p], outs[0].at[:, units(p), :], bsem.at[p])

    def store(p, half):
        return pltpu.make_async_copy(
            obuf.at[p, :, half * SH : (half + 1) * SH, :], outs[2 * p + half], ssem.at[p, half]
        )

    if part:
        z = z_in
    else:
        z_load = pltpu.make_async_copy(z_in, z, zsem)
        z_load.start()
    for k in range(2 * pairs):
        fetch(k, k // 2).start()
    if part:
        for p in range(pairs):
            load(p).start()
    if not begin:
        acc_load = pltpu.make_async_copy(acc_in, acc, asem)
        acc_load.start()
    else:
        acc[...] = jnp.zeros_like(acc)
    router = jnp.zeros((8, PEERS * slots), F32) if begin else router_in[...]
    if not part:
        z_load.wait()

    def block(p, router):
        fetch(0, p).wait()
        fetch(1, p).wait()
        parts, dx, r = expert_block(z, slots, wbuf[p, 0], wbuf[p, 1], wbuf[p, 2])
        if part:
            load(p).wait()
            for k in range(3):
                obuf[p, k] = (parts[k] + stage[p, k]).astype(BF)
            for q in range(pairs):

                @pl.when(p == q)
                def _():
                    for half in range(2):
                        store(q, half).start()
        else:
            for k in range(3):
                stage[p, k] = parts[k]
            store_wide(p).start()
        if not begin:

            @pl.when(p == 0)
            def _():
                acc_load.wait()

        acc[...] += dx
        return router + r

    router = block(0, router) if pairs == 1 else lax.fori_loop(0, pairs, block, router)
    if end:
        rows = acc[...].astype(BF).reshape(PEERS, slots, DS)
        for g in range(slots // EXTRA):
            dbuf[:, :, g * DS : (g + 1) * DS] = rows[:, g * EXTRA : (g + 1) * EXTRA, :]
        if last:
            router_rows(dbuf, slots // EXTRA * DS, router_first[...], router)
        save = pltpu.make_async_copy(dbuf, dx_out, asem)
    else:
        save = pltpu.make_async_copy(acc, dx_out, asem)
    save.start()
    if not last:
        router_out[...] = router
    for p in range(pairs):
        if part:
            store(p, 0).wait()
            store(p, 1).wait()
        else:
            store_wide(p).wait()
    save.wait()


def expert_part(part, z, weights, before=None, at=0, carry=None, end=False, first=None):
    pairs = len(weights) // 2
    last = part == 1 and end
    slots = SLOTS[part]
    rows = PEERS * slots
    width = slots // EXTRA * DS + (128 if last else 0)
    args = [z if part else in_hbm(z), *[in_hbm(w) for w in weights]]
    in_specs = [WHOLE if part else HBM] + [HBM] * len(weights)
    if part:
        args += [in_hbm(before)]
        in_specs += [HBM]
    if carry is not None:
        args += [in_hbm(carry[0]), carry[1]]
        in_specs += [HBM, WHOLE]
    if last:
        args += [first]
        in_specs += [WHOLE]
    if part:
        out_shape = [pltpu.HBM((3, SH, DS), BF)] * (2 * pairs)
    else:
        out_shape = [pltpu.HBM((3, pairs * UNITS, DS), F32)]
    if end:
        out_shape += [pltpu.HBM((PEERS, EXTRA, width), BF)]
    else:
        out_shape += [pltpu.HBM((rows, DS), F32)]
    out_specs = [HBM] * len(out_shape)
    if not last:
        out_shape += [jax.ShapeDtypeStruct((8, rows), F32)]
        out_specs += [WHOLE]
    return pl.pallas_call(
        functools.partial(
            expert_kernel, part=part, pairs=pairs, first=at, begin=carry is None, end=end
        ),
        in_specs=in_specs,
        out_specs=out_specs,
        out_shape=out_shape,
        scratch_shapes=[
            pltpu.VMEM((8, 128, 128) if part else (PEERS, 2 * slots, DS), BF),
            pltpu.VMEM((rows, DS), F32),
            pltpu.VMEM((pairs, 3, UNITS, DS), BF),
            pltpu.VMEM((pairs, 3, UNITS, DS), F32),
            pltpu.VMEM((pairs, 3, UNITS, DS) if part else (8, 128), BF),
            pltpu.VMEM((PEERS, EXTRA, width) if end else (8, 128), BF),
            pltpu.SemaphoreType.DMA,
            pltpu.SemaphoreType.DMA,
            pltpu.SemaphoreType.DMA((pairs, 2)),
            pltpu.SemaphoreType.DMA((pairs,)),
            pltpu.SemaphoreType.DMA((pairs, 2)),
        ],
        compiler_params=params(44),
    )(*args)


def picks(codes, part, start, count):
    rows = PEERS * SLOTS[part]
    row = lax.broadcasted_iota(jnp.int32, (count, rows), 1) + part * PEERS * SLOTS[0]
    code0, code1 = (c[start : start + count] for c in codes)
    return jnp.where((row == code0) | (row == code1), 1.0, 0.0).astype(BF)


def columns(table):
    cols = jnp.transpose(table[...])
    whole = lambda k: cols[:, k : k + 1].astype(jnp.int32)
    return (whole(0), whole(1)), (cols[:, 2:3], cols[:, 3:4]), (whole(4), whole(5)), (whole(6), whole(7))


def slot_rows(back, part):
    slots = SLOTS[part]
    groups = [back[:, :, g * DS : (g + 1) * DS] for g in range(slots // EXTRA)]
    return jnp.concatenate(groups, axis=1).reshape(PEERS * slots, DS)


def combine_first_kernel(table, back, out):
    codes = columns(table)[0]
    rows = slot_rows(back, 0)
    count = 256
    for b in range(SUBS // count):
        out[b * count : (b + 1) * count, :] = contract(
            picks(codes, 0, b * count, count), rows, 1, 0
        )


def combine_last_kernel(table, part, back, out, probs):
    codes, weight, peer, slot = columns(table)
    rows = slot_rows(back, 1)
    count = 256
    n = count // 128
    for b in range(SUBS // count):
        got = contract(picks(codes, 1, b * count, count), rows, 1, 0)
        got = (got + part[b * count : (b + 1) * count, :]).astype(BF)
        for k in range(n):
            h = b * n + k
            out[:, h * DS : (h + 1) * DS] = got[k * 128 : (k + 1) * 128]
    at = SLOTS[1] // EXTRA * DS
    routers = back[:, :, at : at + 128].reshape(PEERS * EXTRA, 128)
    source = lax.broadcasted_iota(jnp.int32, (SUBS, PEERS * EXTRA), 1)
    lane = lax.broadcasted_iota(jnp.int32, (SUBS, 128), 1)
    found = []
    for k in range(2):
        pick = jnp.where(source == peer[k] * EXTRA, 1.0, 0.0).astype(BF)
        line = contract(pick, routers, 1, 0)
        value = jnp.sum(jnp.where(lane == slot[k], line, 0.0), axis=1, keepdims=True)
        found.append(value / weight[k])
    both = jnp.where(lane == 0, found[0], jnp.where(lane == 1, found[1], 0.0))
    probs[...] = jnp.transpose(both)[0:8, :]


def combine_first(table, back):
    return pl.pallas_call(
        combine_first_kernel,
        out_shape=jax.ShapeDtypeStruct((SUBS, DS), F32),
        compiler_params=params(),
        name="combine_first",
    )(table, in_hbm(back))


def combine_last(table, part, back):
    return pl.pallas_call(
        combine_last_kernel,
        out_shape=[
            jax.ShapeDtypeStruct((SUBS // H, H * DS), BF),
            jax.ShapeDtypeStruct((8, SUBS), F32),
        ],
        compiler_params=params(),
        name="combine_last",
    )(table, part, back)


def place(sources, grad_in, grad_out, at, sems):
    copies = []
    start = 0
    for i, source in enumerate(sources):
        here = pl.ds(start, source.shape[1])
        start += source.shape[1]
        copies += [
            pltpu.make_async_copy(source.at[0:2], grad_in.at[at, :, here, :], sems.at[i, 0]),
            pltpu.make_async_copy(source.at[2], grad_out.at[at, here, :], sems.at[i, 1]),
        ]
    for c in copies:
        c.start()
    for c in copies:
        c.wait()


def final_own_kernel(which, own0, own1, own2, own3, grad_in, grad_out, total, sems):
    for k in range(3):
        value = own0[k].astype(F32) + own1[k].astype(F32) + own2[k].astype(F32)
        total[k] = (value + own3[k].astype(F32)).astype(BF)
    place([total], grad_in, grad_out, which[0], sems)


def final_other_kernel(which, other, _in, _out, grad_in, grad_out, sems):
    place([other], grad_in, grad_out, 1 - which[0], sems)


def final(which, own, other):
    smem = pl.BlockSpec(memory_space=pltpu.SMEM)
    out_shape = [pltpu.HBM((2, 2, SH, DS), BF), pltpu.HBM((2, SH, DS), BF)]
    grads = pl.pallas_call(
        final_own_kernel,
        in_specs=[smem] + [WHOLE] * 4,
        out_specs=[HBM, HBM],
        out_shape=out_shape,
        scratch_shapes=[pltpu.VMEM((3, SH, DS), BF), pltpu.SemaphoreType.DMA((1, 2))],
        compiler_params=params(),
        name="final_own",
    )(which, *own)
    return pl.pallas_call(
        final_other_kernel,
        in_specs=[smem, WHOLE, HBM, HBM],
        out_specs=[HBM, HBM],
        out_shape=out_shape,
        input_output_aliases={2: 0, 3: 1},
        scratch_shapes=[pltpu.SemaphoreType.DMA((1, 2))],
        compiler_params=params(),
        name="final_other",
    )(which, other, *[in_hbm(g) for g in grads])


def ring(a, step):
    return lax.ppermute(a, "x", [(i, (i + step) % 4) for i in range(4)])


def swap(a):
    return lax.ppermute(a, "yh", [(0, 1), (1, 0)])


def exchange(a):
    return lax.all_to_all(a, PLANE, 0, 0, tiled=True)


def add(*arrays):
    return sum(a.astype(F32) for a in arrays).astype(BF)


def layer(tokens, cotangent, expert_ids, slot_ids, route_probs, weights_in, weights_out):
    yh = lax.axis_index("yh")
    both = jnp.concatenate([weights_in, weights_out[:, None]], axis=1)
    w_p = swap(jnp.where(yh == 0, both[1], both[0]))
    w_o = jnp.where(yh == 0, both[0], both[1])
    w_o_m = ring(w_o, 1)
    w_o_p = ring(w_o, -1)
    w_p_m = ring(w_p, 1)
    w_p_p = ring(w_p, -1)
    w_o_2 = ring(w_o_p, -1)
    w_p_2 = ring(w_p_m, 1)

    dest = expert_ids % 2 * (PEERS // 2) + expert_ids // 2
    code = jnp.where(
        slot_ids < SLOTS[0],
        dest * SLOTS[0] + slot_ids,
        PEERS * SLOTS[0] + dest * SLOTS[1] + slot_ids - SLOTS[0],
    )
    table = [code, route_probs, dest, slot_ids]
    table = jnp.concatenate([t.astype(F32) for t in table], axis=2)
    table = jnp.transpose(table, (2, 1, 0)).reshape(8, SUBS)

    z1 = exchange(dispatch(table, tokens, cotangent, 0))
    z2 = exchange(dispatch(table, tokens, cotangent, 1))

    near = [w_p_p, w_p_m, w_o_p, w_o_m]
    far = [w_p_2, w_o_2]
    own = [w_p, w_o]
    dw_near, *carry = expert_part(0, z1, near)
    dw_rest, back1, router1 = expert_part(0, z1, far + own, carry=carry, end=True)
    back1 = exchange(back1)
    p_2, o_2, *carry = expert_part(1, z2, far, dw_rest, 0)
    p_2 = ring(p_2, 2)
    o_2 = ring(o_2, 2)
    p_p, p_m, o_p, o_m, *carry = expert_part(1, z2, near, dw_near, 0, carry)
    p_p = ring(p_p, 1)
    p_m = ring(p_m, -1)
    o_p = ring(o_p, 1)
    o_m = ring(o_m, -1)
    p_0, o_0, back2 = expert_part(1, z2, own, dw_rest, 1, carry, True, router1)
    back2 = exchange(back2)
    other = swap(add(p_0, p_p, p_m, p_2))
    grad_in, grad_out = final(yh.astype(jnp.int32).reshape(1), (o_0, o_p, o_m, o_2), other)

    part = combine_first(table, back1)
    grad_tokens, probs = combine_last(table, part, back2)
    grad_probs = jnp.transpose(probs[0:2].reshape(2, H, SUBS // H), (2, 1, 0))
    return grad_tokens, grad_probs, grad_in, grad_out


def solution(mesh):
    wide = Mesh(mesh.devices.reshape(4, 2, 4, 2, 2), AXES)
    dp = ("x", "yh")
    expert = ("z", "yl", "core")
    rows2 = P(AXES, None)
    rows3 = P(AXES, None, None)
    w_in = P(expert, None, dp, None)
    w_out = P(expert, dp, None)
    return jax.shard_map(
        layer,
        mesh=wide,
        in_specs=(rows2, rows2, rows3, rows3, rows3, w_in, w_out),
        out_specs=(rows2, rows3, w_in, w_out),
        check_vma=False,
    )
```

profile of v0, /device:TPU:0, one launch (start us, length us, event | category | flops | bytes accessed | tf_op | source)
XLA Modules:
  0.0 230.2 jit_solution(17360045643992942504)
XLA Ops:
  0.6 0.8 fusion.1
  1.5 0.7 convert_element_type.28
  2.2 1.2 copy-done
  3.4 1.2 copy-done.2
  4.6 4.3 %shard_map.102 = bf16[32,80,512]{2,1,0:T(8,128)(2,1)} custom-call(f32[8,1024]{1,0:T(8,128)S(1)} %maximum_bitcast_fusion.table, bf16[128,4096]{1,0:T(8,128)(2,1)S(1)} %copy-done, bf16[128,4096]{1,0:T(8,128)(2,1)S(1)} %copy-done.2), custom_call_target="tpu_custom_call" | custom-call | tf_op jit(solution)/shard_map/pallas_call | solution.py:59
  8.9 8.4 %all-to-all-start = ((bf16[32,80,512]{2,1,0:T(8,128)(2,1)}), bf16[32,80,512]{2,1,0:T(8,128)(2,1)S(1)}, u32[]{:S(2)}, u32[]{:S(2)}) async-start(bf16[32,80,512]{2,1,0:T(8,128)(2,1)} %shard_map.102), calls=%async_computation | async-start | bytes 5242880 | tf_op jit(solution)/shard_map/all_to_all | solution.py:405
  17.4 2.7 %select_bitcast_fusion = (bf16[3,224,512]{2,1,0:T(8,128)(2,1)S(1)}, bf16[3,224,512]{2,1,0:T(8,128)(2,1)}) fusion(pred[]{:T(512)S(6)} %eq.6, bf16[2,1,224,512]{3,2,1,0:T(8,128)(2,1)} %bitcast.14, bf16[2,2,224,512]{3,2,1,0:T(8,128)(2,1)} %param.12), kind=kLoop, calls=%fused_computation.5 | loop fusion | flops 1720320 | bytes 2752513 | tf_op jit(solution)/shard_map/jit(_where)/select_n | solution.py:416
  20.1 3.3 %collective-permute-start = (bf16[3,224,512]{2,1,0:T(8,128)(2,1)}, bf16[3,224,512]{2,1,0:T(8,128)(2,1)}, u32[]{:S(2)}, u32[]{:S(2)}) collective-permute-start(bf16[3,224,512]{2,1,0:T(8,128)(2,1)} %get-tuple-element.57), channel_id=1, source_target_pairs={{0,16},{16,0},{1,17},{17,1},{2,18},{18,2},{3,19},{19,3},{4,20},{20... | collective-permute-start | bytes 2064392 | tf_op jit(solution)/shard_map/ppermute | solution.py:401
  23.4 3.3 %shard_map.105 = bf16[32,48,512]{2,1,0:T(8,128)(2,1)} custom-call(f32[8,1024]{1,0:T(8,128)S(1)} %maximum_bitcast_fusion.table, bf16[128,4096]{1,0:T(8,128)(2,1)S(1)} %copy-done.1, bf16[128,4096]{1,0:T(8,128)(2,1)S(1)} %copy-done.3), custom_call_target="tpu_custom_call" | custom-call | tf_op jit(solution)/shard_map/pallas_call | solution.py:59
  26.7 24.1 %all-to-all-done.refs_0_ = bf16[32,80,512]{2,1,0:T(8,128)(2,1)S(1)} async-done(((bf16[32,80,512]{2,1,0:T(8,128)(2,1)}), bf16[32,80,512]{2,1,0:T(8,128)(2,1)S(1)}, u32[]{:S(2)}, u32[]{:S(2)}) %all-to-all-start) | async-done | bytes 2621472 | tf_op jit(solution)/shard_map/all_to_all | solution.py:405
  50.9 1.6 copy-done.5
  52.4 7.4 %all-to-all-start.2 = ((bf16[32,48,512]{2,1,0:T(8,128)(2,1)}), bf16[32,48,512]{2,1,0:T(8,128)(2,1)S(1)}, u32[]{:S(2)}, u32[]{:S(2)}) async-start(bf16[32,48,512]{2,1,0:T(8,128)(2,1)} %shard_map.105), calls=%async_computation.2 | async-start | bytes 3145728 | tf_op jit(solution)/shard_map/all_to_all | solution.py:405
  59.9 2.8 %collective-permute-start.3 = (bf16[3,224,512]{2,1,0:T(8,128)(2,1)S(1)}, bf16[3,224,512]{2,1,0:T(8,128)(2,1)S(1)}, u32[]{:S(2)}, u32[]{:S(2)}) collective-permute-start(bf16[3,224,512]{2,1,0:T(8,128)(2,1)S(1)} %get-tuple-element.56.refs_4_.refs_2_), channel_id=1, source_target_pairs={{0,96},{32,0},{64,32},{96,64},{1,97},{33,1},{65,33},{97,65},{2,98}... | collective-permute-start | bytes 2064392 | tf_op jit(solution)/shard_map/ppermute | solution.py:397
  62.7 2.9 %collective-permute-done.refs_3_.refs_1_ = bf16[3,224,512]{2,1,0:T(8,128)(2,1)} collective-permute-done((bf16[3,224,512]{2,1,0:T(8,128)(2,1)}, bf16[3,224,512]{2,1,0:T(8,128)(2,1)}, u32[]{:S(2)}, u32[]{:S(2)}) %collective-permute-start) | collective-permute-done | bytes 688160 | tf_op jit(solution)/shard_map/ppermute | solution.py:401
  65.6 1.5 collective-permute-start.1
  67.1 1.5 collective-permute-start.6
  68.6 1.7 collective-permute-start.5
  70.4 8.1 %collective-permute-done.3.refs_3_ = bf16[3,224,512]{2,1,0:T(8,128)(2,1)S(1)} collective-permute-done((bf16[3,224,512]{2,1,0:T(8,128)(2,1)S(1)}, bf16[3,224,512]{2,1,0:T(8,128)(2,1)S(1)}, u32[]{:S(2)}, u32[]{:S(2)}) %collective-permute-start.3) | collective-permute-done | bytes 688160 | tf_op jit(solution)/shard_map/ppermute | solution.py:397
  78.5 3.7 %collective-permute-start.4 = (bf16[3,224,512]{2,1,0:T(8,128)(2,1)S(1)}, bf16[3,224,512]{2,1,0:T(8,128)(2,1)S(1)}, u32[]{:S(2)}, u32[]{:S(2)}) collective-permute-start(bf16[3,224,512]{2,1,0:T(8,128)(2,1)S(1)} %collective-permute-done.3.refs_3_), channel_id=1, source_target_pairs={{0,96},{32,0},{64,32},{96,64},{1,97},{33,1},{65,33},{97,65},{2,98}... | collective-permute-start | bytes 2064392 | tf_op jit(solution)/shard_map/ppermute | solution.py:397
  82.2 3.2 %collective-permute-done.1.refs_2_ = bf16[3,224,512]{2,1,0:T(8,128)(2,1)S(1)} collective-permute-done((bf16[3,224,512]{2,1,0:T(8,128)(2,1)}, bf16[3,224,512]{2,1,0:T(8,128)(2,1)S(1)}, u32[]{:S(2)}, u32[]{:S(2)}) %collective-permute-start.1) | collective-permute-done | bytes 688160 | tf_op jit(solution)/shard_map/ppermute | solution.py:397
  85.4 0.3 collective-permute-start.2
  85.6 14.5 %collective-permute-done.6.refs_4_ = bf16[3,224,512]{2,1,0:T(8,128)(2,1)S(1)} collective-permute-done((bf16[3,224,512]{2,1,0:T(8,128)(2,1)S(1)}, bf16[3,224,512]{2,1,0:T(8,128)(2,1)S(1)}, u32[]{:S(2)}, u32[]{:S(2)}) %collective-permute-start.6) | collective-permute-done | bytes 688160 | tf_op jit(solution)/shard_map/ppermute | solution.py:397
  100.1 0.9 copy-done.10
  101.0 0.9 copy-done.11
  101.8 14.8 %shard_map.103 = (f32[3,896,512]{2,1,0:T(8,128)}, f32[1280,512]{1,0:T(8,128)}, f32[8,1280]{1,0:T(8,128)S(1)}) custom-call(bf16[32,80,512]{2,1,0:T(8,128)(2,1)} %copy-done.5, bf16[3,224,512]{2,1,0:T(8,128)(2,1)} %copy-done.11, bf16[3,224,512]{2,1,0:T(8,128)(2,1)} %copy-done.9, bf16[3,224,512]{2,1,0:T(8,128)(2,1)} %copy-done.8, bf16[3,224,512]{2,1,0:T(8,128)(2,1)} %copy-done.10), custom_call_target="tpu_custom_call" | custom-call | tf_op jit(solution)/shard_map/pallas_call | solution.py:246
  116.7 0.8 copy-done.12
  117.8 15.0 %shard_map.104 = (f32[3,896,512]{2,1,0:T(8,128)}, bf16[32,8,2560]{2,1,0:T(8,128)(2,1)}, f32[8,1280]{1,0:T(8,128)S(1)}) custom-call(bf16[32,80,512]{2,1,0:T(8,128)(2,1)} %copy-done.5, bf16[3,224,512]{2,1,0:T(8,128)(2,1)} %copy-done.13, bf16[3,224,512]{2,1,0:T(8,128)(2,1)} %copy-done.12, bf16[3,224,512]{2,1,0:T(8,128)(2,1)} %collective-permute-done.refs_3_.refs_1_, ...), custom_call_target="tpu_custom_call" | custom-call | tf_op jit(solution)/shard_map/pallas_call | solution.py:246
  132.8 7.8 %all-to-all-start.1 = ((bf16[32,8,2560]{2,1,0:T(8,128)(2,1)}), bf16[32,8,2560]{2,1,0:T(8,128)(2,1)S(1)}, u32[]{:S(2)}, u32[]{:S(2)}) async-start(bf16[32,8,2560]{2,1,0:T(8,128)(2,1)} %get-tuple-element.31), calls=%async_computation.1 | async-start | bytes 2621440 | tf_op jit(solution)/shard_map/all_to_all | solution.py:405
  140.6 6.6 %shard_map.106 = (bf16[3,224,512]{2,1,0:T(8,128)(2,1)}, bf16[3,224,512]{2,1,0:T(8,128)(2,1)}, f32[768,512]{1,0:T(8,128)}, f32[8,768]{1,0:T(8,128)S(1)}) custom-call(bf16[32,48,512]{2,1,0:T(8,128)(2,1)S(1)} %all-to-all-done.2.refs_0_, bf16[3,224,512]{2,1,0:T(8,128)(2,1)} %copy-done.13, bf16[3,224,512]{2,1,0:T(8,128)(2,1)} %copy-done.12, ...), custom_call_target="tpu_custom_call" | custom-call | tf_op jit(solution)/shard_map/pallas_call | solution.py:246
  147.2 10.3 %shard_map.107 = (bf16[3,224,512]{2,1,0:T(8,128)(2,1)}, bf16[3,224,512]{2,1,0:T(8,128)(2,1)}, bf16[3,224,512]{2,1,0:T(8,128)(2,1)}, bf16[3,224,512]{2,1,0:T(8,12...) custom-call(bf16[32,48,512]{2,1,0:T(8,128)(2,1)S(1)} %all-to-all-done.2.refs_0_, bf16[3,224,512]{2,1,0:T(8,128)(2,1)} %copy-done.11, ...), custom_call_target="tpu_custom_call" | custom-call | tf_op jit(solution)/shard_map/pallas_call | solution.py:246
  157.5 0.3 collective-permute-start.7
  157.8 3.0 %collective-permute-start.8 = (bf16[3,224,512]{2,1,0:T(8,128)(2,1)}, bf16[3,224,512]{2,1,0:T(8,128)(2,1)}, u32[]{:S(2)}, u32[]{:S(2)}) collective-permute-start(bf16[3,224,512]{2,1,0:T(8,128)(2,1)} %get-tuple-element.44), channel_id=1, source_target_pairs={{0,96},{32,0},{64,32},{96,64},{1,97},{33,1},{65,33},{97,65},{2,98}... | collective-permute-start | bytes 2064392 | tf_op jit(solution)/shard_map/ppermute | solution.py:397
  160.8 0.6 collective-permute-start.9
  161.4 6.6 %shard_map.108 = (bf16[3,224,512]{2,1,0:T(8,128)(2,1)}, bf16[3,224,512]{2,1,0:T(8,128)(2,1)}, bf16[32,8,1664]{2,1,0:T(8,128)(2,1)}) custom-call(bf16[32,48,512]{2,1,0:T(8,128)(2,1)S(1)} %all-to-all-done.2.refs_0_, bf16[3,224,512]{2,1,0:T(8,128)(2,1)} %collective-permute-done.refs_3_.refs_1_, bf16[3,224,512]{2,1,0:T(8,128)(2,1)} %copy-done.6, ...), custom_call_target="tpu_custom_call" | custom-call | tf_op jit(solution)/shard_map/pallas_call | solution.py:246
  168.0 7.3 %all-to-all-start.3 = ((bf16[32,8,1664]{2,1,0:T(8,128)(2,1)}), bf16[32,8,1664]{2,1,0:T(8,128)(2,1)S(1)}, u32[]{:S(2)}, u32[]{:S(2)}) async-start(bf16[32,8,1664]{2,1,0:T(8,128)(2,1)} %get-tuple-element.39), calls=%async_computation.3 | async-start | bytes 1703936 | tf_op jit(solution)/shard_map/all_to_all | solution.py:405
  175.4 0.7 collective-permute-start.11
  176.1 2.6 %collective-permute-start.12 = (bf16[3,224,512]{2,1,0:T(8,128)(2,1)}, bf16[3,224,512]{2,1,0:T(8,128)(2,1)S(1)}, u32[]{:S(2)}, u32[]{:S(2)}) collective-permute-start(bf16[3,224,512]{2,1,0:T(8,128)(2,1)} %get-tuple-element.48), channel_id=1, source_target_pairs={{0,96},{32,0},{64,32},{96,64},{1,97},{33,1},{65,33},{97,65},{2,98}... | collective-permute-start | bytes 2064392 | tf_op jit(solution)/shard_map/ppermute | solution.py:397
  178.7 12.0 %collective-permute-done.7 = bf16[3,224,512]{2,1,0:T(8,128)(2,1)} collective-permute-done((bf16[3,224,512]{2,1,0:T(8,128)(2,1)}, bf16[3,224,512]{2,1,0:T(8,128)(2,1)}, u32[]{:S(2)}, u32[]{:S(2)}) %collective-permute-start.7) | collective-permute-done | bytes 688160 | tf_op jit(solution)/shard_map/ppermute | solution.py:397
  190.7 0.9 collective-permute-done.8
  191.7 0.3 collective-permute-done.9
  191.9 2.8 %add_convert_fusion = bf16[3,224,512]{2,1,0:T(8,128)(2,1)} fusion(bf16[3,224,512]{2,1,0:T(8,128)(2,1)} %collective-permute-done.9, bf16[3,224,512]{2,1,0:T(8,128)(2,1)} %collective-permute-done.8, bf16[3,224,512]{2,1,0:T(8,128)(2,1)} %collective-permute-done.7, bf16[3,224,512]{2,1,0:T(8,128)(2,1)S(1)} %copy-done.14), kind=kLoop, calls=%fused_computation.2 | loop fusion | flops 2752512 | bytes 3440640 | tf_op jit(solution)/shard_map/convert_element_type | solution.py:409
  194.7 3.1 %collective-permute-start.10 = (bf16[3,224,512]{2,1,0:T(8,128)(2,1)}, bf16[3,224,512]{2,1,0:T(8,128)(2,1)}, u32[]{:S(2)}, u32[]{:S(2)}) collective-permute-start(bf16[3,224,512]{2,1,0:T(8,128)(2,1)} %add_convert_fusion), channel_id=1, source_target_pairs={{0,16},{16,0},{1,17},{17,1},{2,18},{18,2},{3,19},{19,3},{4,20},{20... | collective-permute-start | bytes 2064392 | tf_op jit(solution)/shard_map/ppermute | solution.py:401
  197.8 22.7 %collective-permute-done.11.own1 = bf16[3,224,512]{2,1,0:T(8,128)(2,1)S(1)} collective-permute-done((bf16[3,224,512]{2,1,0:T(8,128)(2,1)}, bf16[3,224,512]{2,1,0:T(8,128)(2,1)S(1)}, u32[]{:S(2)}, u32[]{:S(2)}) %collective-permute-start.11) | collective-permute-done | bytes 688160 | tf_op jit(solution)/shard_map/ppermute | solution.py:397
  220.6 1.2 final_own.1
  221.8 3.2 %combine_first.1.part = f32[1024,512]{1,0:T(8,128)S(1)} custom-call(f32[8,1024]{1,0:T(8,128)S(1)} %maximum_bitcast_fusion.table, bf16[32,8,2560]{2,1,0:T(8,128)(2,1)} %copy-done.7), custom_call_target="tpu_custom_call" | custom-call | tf_op jit(solution)/shard_map/combine_first/pallas_call | solution.py:325
  225.0 2.4 %combine_last.1 = (bf16[128,4096]{1,0:T(8,128)(2,1)}, f32[8,1024]{1,0:T(8,128)S(1)}) custom-call(f32[8,1024]{1,0:T(8,128)S(1)} %maximum_bitcast_fusion.table, f32[1024,512]{1,0:T(8,128)S(1)} %combine_first.1.part, bf16[32,8,1664]{2,1,0:T(8,128)(2,1)S(1)} %all-to-all-done.3.back), custom_call_target="tpu_custom_call" | custom-call | tf_op jit(solution)/shard_map/combine_last/pallas_call | solution.py:334
  227.4 0.6 slice_bitcast_fusion
  228.0 2.0 final_other.1
  (36 shorter events, 0.3 us)
Async XLA Ops:
  2.2 1.2 copy-start
  3.4 1.2 copy-start.2
  8.9 41.9 %all-to-all-start = ((bf16[32,80,512]{2,1,0:T(8,128)(2,1)}), bf16[32,80,512]{2,1,0:T(8,128)(2,1)S(1)}, u32[]{:S(2)}, u32[]{:S(2)}) async-start(bf16[32,80,512]{2,1,0:T(8,128)(2,1)} %shard_map.102), calls=%async_computation | async-start | bytes 5242880 | tf_op jit(solution)/shard_map/all_to_all | solution.py:405
  17.4 6.0 %copy-start.1 = (bf16[128,4096]{1,0:T(8,128)(2,1)S(1)}, bf16[128,4096]{1,0:T(8,128)(2,1)}, u32[]{:S(2)}) copy-start(bf16[128,4096]{1,0:T(8,128)(2,1)} %tok.3) | copy-start | bytes 3145732
  17.4 6.0 %copy-start.3 = (bf16[128,4096]{1,0:T(8,128)(2,1)S(1)}, bf16[128,4096]{1,0:T(8,128)(2,1)}, u32[]{:S(2)}) copy-start(bf16[128,4096]{1,0:T(8,128)(2,1)} %cot.3) | copy-start | bytes 3145732
  20.1 47.0 %copy-start.6 = (bf16[3,224,512]{2,1,0:T(8,128)(2,1)}, bf16[3,224,512]{2,1,0:T(8,128)(2,1)S(1)}, u32[]{:S(2)}) copy-start(bf16[3,224,512]{2,1,0:T(8,128)(2,1)S(1)} %get-tuple-element.56.refs_4_.refs_2_) | copy-start | bytes 2064388
  20.1 45.5 %collective-permute-start = (bf16[3,224,512]{2,1,0:T(8,128)(2,1)}, bf16[3,224,512]{2,1,0:T(8,128)(2,1)}, u32[]{:S(2)}, u32[]{:S(2)}) collective-permute-start(bf16[3,224,512]{2,1,0:T(8,128)(2,1)} %get-tuple-element.57), channel_id=1, source_target_pairs={{0,16},{16,0},{1,17},{17,1},{2,18},{18,2},{3,19},{19,3},{4,20},{20... | collective-permute-start | bytes 2064392 | tf_op jit(solution)/shard_map/ppermute | solution.py:401
  50.9 1.6 copy-start.5
  52.4 80.4 %all-to-all-start.2 = ((bf16[32,48,512]{2,1,0:T(8,128)(2,1)}), bf16[32,48,512]{2,1,0:T(8,128)(2,1)S(1)}, u32[]{:S(2)}, u32[]{:S(2)}) async-start(bf16[32,48,512]{2,1,0:T(8,128)(2,1)} %shard_map.105), calls=%async_computation.2 | async-start | bytes 3145728 | tf_op jit(solution)/shard_map/all_to_all | solution.py:405
  59.9 18.6 %collective-permute-start.3 = (bf16[3,224,512]{2,1,0:T(8,128)(2,1)S(1)}, bf16[3,224,512]{2,1,0:T(8,128)(2,1)S(1)}, u32[]{:S(2)}, u32[]{:S(2)}) collective-permute-start(bf16[3,224,512]{2,1,0:T(8,128)(2,1)S(1)} %get-tuple-element.56.refs_4_.refs_2_), channel_id=1, source_target_pairs={{0,96},{32,0},{64,32},{96,64},{1,97},{33,1},{65,33},{97,65},{2,98}... | collective-permute-start | bytes 2064392 | tf_op jit(solution)/shard_map/ppermute | solution.py:397
  65.6 19.7 %collective-permute-start.1 = (bf16[3,224,512]{2,1,0:T(8,128)(2,1)}, bf16[3,224,512]{2,1,0:T(8,128)(2,1)S(1)}, u32[]{:S(2)}, u32[]{:S(2)}) collective-permute-start(bf16[3,224,512]{2,1,0:T(8,128)(2,1)} %collective-permute-done.refs_3_.refs_1_), channel_id=1, source_target_pairs={{0,32},{32,64},{64,96},{96,0},{1,33},{33,65},{65,97},{97,1},{2,34}... | collective-permute-start | bytes 2064392 | tf_op jit(solution)/shard_map/ppermute | solution.py:397
  67.1 33.0 %collective-permute-start.6 = (bf16[3,224,512]{2,1,0:T(8,128)(2,1)S(1)}, bf16[3,224,512]{2,1,0:T(8,128)(2,1)S(1)}, u32[]{:S(2)}, u32[]{:S(2)}) collective-permute-start(bf16[3,224,512]{2,1,0:T(8,128)(2,1)S(1)} %get-tuple-element.56.refs_4_.refs_2_), channel_id=1, source_target_pairs={{0,32},{32,64},{64,96},{96,0},{1,33},{33,65},{65,97},{97,1},{2,34}... | collective-permute-start | bytes 2064392 | tf_op jit(solution)/shard_map/ppermute | solution.py:397
  68.6 31.5 %collective-permute-start.5 = (bf16[3,224,512]{2,1,0:T(8,128)(2,1)}, bf16[3,224,512]{2,1,0:T(8,128)(2,1)S(1)}, u32[]{:S(2)}, u32[]{:S(2)}) collective-permute-start(bf16[3,224,512]{2,1,0:T(8,128)(2,1)} %collective-permute-done.refs_3_.refs_1_), channel_id=1, source_target_pairs={{0,96},{32,0},{64,32},{96,64},{1,97},{33,1},{65,33},{97,65},{2,98}... | collective-permute-start | bytes 2064392 | tf_op jit(solution)/shard_map/ppermute | solution.py:397
  78.5 21.6 %copy-start.8 = (bf16[3,224,512]{2,1,0:T(8,128)(2,1)}, bf16[3,224,512]{2,1,0:T(8,128)(2,1)S(1)}, u32[]{:S(2)}) copy-start(bf16[3,224,512]{2,1,0:T(8,128)(2,1)S(1)} %collective-permute-done.3.refs_3_) | copy-start | bytes 2064388
  78.5 38.2 %collective-permute-start.4 = (bf16[3,224,512]{2,1,0:T(8,128)(2,1)S(1)}, bf16[3,224,512]{2,1,0:T(8,128)(2,1)S(1)}, u32[]{:S(2)}, u32[]{:S(2)}) collective-permute-start(bf16[3,224,512]{2,1,0:T(8,128)(2,1)S(1)} %collective-permute-done.3.refs_3_), channel_id=1, source_target_pairs={{0,96},{32,0},{64,32},{96,64},{1,97},{33,1},{65,33},{97,65},{2,98}... | collective-permute-start | bytes 2064392 | tf_op jit(solution)/shard_map/ppermute | solution.py:397
  85.4 14.8 %copy-start.9 = (bf16[3,224,512]{2,1,0:T(8,128)(2,1)}, bf16[3,224,512]{2,1,0:T(8,128)(2,1)S(1)}, u32[]{:S(2)}) copy-start(bf16[3,224,512]{2,1,0:T(8,128)(2,1)S(1)} %collective-permute-done.1.refs_2_) | copy-start | bytes 2064388
  85.4 31.3 %collective-permute-start.2 = (bf16[3,224,512]{2,1,0:T(8,128)(2,1)S(1)}, bf16[3,224,512]{2,1,0:T(8,128)(2,1)S(1)}, u32[]{:S(2)}, u32[]{:S(2)}) collective-permute-start(bf16[3,224,512]{2,1,0:T(8,128)(2,1)S(1)} %collective-permute-done.1.refs_2_), channel_id=1, source_target_pairs={{0,32},{32,64},{64,96},{96,0},{1,33},{33,65},{65,97},{97,1},{2,34}... | collective-permute-start | bytes 2064392 | tf_op jit(solution)/shard_map/ppermute | solution.py:397
  100.1 0.9 copy-start.10
  101.0 0.9 copy-start.11
  116.7 0.8 copy-start.12
  116.7 1.1 copy-start.13
  132.8 35.2 %all-to-all-start.1 = ((bf16[32,8,2560]{2,1,0:T(8,128)(2,1)}), bf16[32,8,2560]{2,1,0:T(8,128)(2,1)S(1)}, u32[]{:S(2)}, u32[]{:S(2)}) async-start(bf16[32,8,2560]{2,1,0:T(8,128)(2,1)} %get-tuple-element.31), calls=%async_computation.1 | async-start | bytes 2621440 | tf_op jit(solution)/shard_map/all_to_all | solution.py:405
  157.5 33.3 %collective-permute-start.7 = (bf16[3,224,512]{2,1,0:T(8,128)(2,1)}, bf16[3,224,512]{2,1,0:T(8,128)(2,1)}, u32[]{:S(2)}, u32[]{:S(2)}) collective-permute-start(bf16[3,224,512]{2,1,0:T(8,128)(2,1)} %get-tuple-element.43), channel_id=1, source_target_pairs={{0,32},{32,64},{64,96},{96,0},{1,33},{33,65},{65,97},{97,1},{2,34}... | collective-permute-start | bytes 2064392 | tf_op jit(solution)/shard_map/ppermute | solution.py:397
  157.8 33.9 %collective-permute-start.8 = (bf16[3,224,512]{2,1,0:T(8,128)(2,1)}, bf16[3,224,512]{2,1,0:T(8,128)(2,1)}, u32[]{:S(2)}, u32[]{:S(2)}) collective-permute-start(bf16[3,224,512]{2,1,0:T(8,128)(2,1)} %get-tuple-element.44), channel_id=1, source_target_pairs={{0,96},{32,0},{64,32},{96,64},{1,97},{33,1},{65,33},{97,65},{2,98}... | collective-permute-start | bytes 2064392 | tf_op jit(solution)/shard_map/ppermute | solution.py:397
  160.8 31.2 %collective-permute-start.9 = (bf16[3,224,512]{2,1,0:T(8,128)(2,1)}, bf16[3,224,512]{2,1,0:T(8,128)(2,1)}, u32[]{:S(2)}, u32[]{:S(2)}) collective-permute-start(bf16[3,224,512]{2,1,0:T(8,128)(2,1)} %get-tuple-element.45), channel_id=1, source_target_pairs={{0,64},{32,96},{64,0},{96,32},{1,65},{33,97},{65,1},{97,33},{2,66}... | collective-permute-start | bytes 2064392 | tf_op jit(solution)/shard_map/ppermute | solution.py:397
  168.0 23.9 %copy-start.14 = (bf16[3,224,512]{2,1,0:T(8,128)(2,1)S(1)}, bf16[3,224,512]{2,1,0:T(8,128)(2,1)}, u32[]{:S(2)}) copy-start(bf16[3,224,512]{2,1,0:T(8,128)(2,1)} %get-tuple-element.42) | copy-start | bytes 2064388
  168.0 26.7 %copy-start.7 = (bf16[32,8,2560]{2,1,0:T(8,128)(2,1)}, bf16[32,8,2560]{2,1,0:T(8,128)(2,1)S(1)}, u32[]{:S(2)}) copy-start(bf16[32,8,2560]{2,1,0:T(8,128)(2,1)S(1)} %all-to-all-done.1.back) | copy-start | bytes 3932164
  168.0 57.0 %all-to-all-start.3 = ((bf16[32,8,1664]{2,1,0:T(8,128)(2,1)}), bf16[32,8,1664]{2,1,0:T(8,128)(2,1)S(1)}, u32[]{:S(2)}, u32[]{:S(2)}) async-start(bf16[32,8,1664]{2,1,0:T(8,128)(2,1)} %get-tuple-element.39), calls=%async_computation.3 | async-start | bytes 1703936 | tf_op jit(solution)/shard_map/all_to_all | solution.py:405
  175.4 45.2 %collective-permute-start.11 = (bf16[3,224,512]{2,1,0:T(8,128)(2,1)}, bf16[3,224,512]{2,1,0:T(8,128)(2,1)S(1)}, u32[]{:S(2)}, u32[]{:S(2)}) collective-permute-start(bf16[3,224,512]{2,1,0:T(8,128)(2,1)} %get-tuple-element.47), channel_id=1, source_target_pairs={{0,32},{32,64},{64,96},{96,0},{1,33},{33,65},{65,97},{97,1},{2,34}... | collective-permute-start | bytes 2064392 | tf_op jit(solution)/shard_map/ppermute | solution.py:397
  176.1 44.5 %collective-permute-start.12 = (bf16[3,224,512]{2,1,0:T(8,128)(2,1)}, bf16[3,224,512]{2,1,0:T(8,128)(2,1)S(1)}, u32[]{:S(2)}, u32[]{:S(2)}) collective-permute-start(bf16[3,224,512]{2,1,0:T(8,128)(2,1)} %get-tuple-element.48), channel_id=1, source_target_pairs={{0,96},{32,0},{64,32},{96,64},{1,97},{33,1},{65,33},{97,65},{2,98}... | collective-permute-start | bytes 2064392 | tf_op jit(solution)/shard_map/ppermute | solution.py:397
  190.7 29.9 %collective-permute-start.13 = (bf16[3,224,512]{2,1,0:T(8,128)(2,1)}, bf16[3,224,512]{2,1,0:T(8,128)(2,1)S(1)}, u32[]{:S(2)}, u32[]{:S(2)}) collective-permute-start(bf16[3,224,512]{2,1,0:T(8,128)(2,1)} %get-tuple-element.49), channel_id=1, source_target_pairs={{0,64},{32,96},{64,0},{96,32},{1,65},{33,97},{65,1},{97,33},{2,66}... | collective-permute-start | bytes 2064392 | tf_op jit(solution)/shard_map/ppermute | solution.py:397
  191.9 28.7 %copy-start.4 = (bf16[3,224,512]{2,1,0:T(8,128)(2,1)S(1)}, bf16[3,224,512]{2,1,0:T(8,128)(2,1)}, u32[]{:S(2)}) copy-start(bf16[3,224,512]{2,1,0:T(8,128)(2,1)} %get-tuple-element.46.own0) | copy-start | bytes 2064388
  194.7 33.3 %collective-permute-start.10 = (bf16[3,224,512]{2,1,0:T(8,128)(2,1)}, bf16[3,224,512]{2,1,0:T(8,128)(2,1)}, u32[]{:S(2)}, u32[]{:S(2)}) collective-permute-start(bf16[3,224,512]{2,1,0:T(8,128)(2,1)} %add_convert_fusion), channel_id=1, source_target_pairs={{0,16},{16,0},{1,17},{17,1},{2,18},{18,2},{3,19},{19,3},{4,20},{20... | collective-permute-start | bytes 2064392 | tf_op jit(solution)/shard_map/ppermute | solution.py:401
where the time goes:
time: 231 us; the launch traced here: 230 us
  waiting for transfers between devices  88.9 us (38%)
  Pallas kernels  69.7 us (30%)
  starting transfers between devices  56.1 us (24%)
  local copies, waits for them, and re-layouts  7.41 us (3%)
  other arithmetic  7.05 us (3%)
    ppermute x12, waiting for transfers between devices, ring(): return lax.ppermute(a, 'x', [(i, (i + step) % 4) for i in range(4)])  61.8 us
    pallas_call x5, Pallas kernels, expert_part(): pl.pallas_call(functools.partial(expert_kernel, part=part, pairs=pairs, f...  53.3 us
    all_to_all x4, starting transfers between devices, exchange(): return lax.all_to_all(a, PLANE, 0, 0, tiled=True)  31 us
    all_to_all x4, waiting for transfers between devices, exchange(): return lax.all_to_all(a, PLANE, 0, 0, tiled=True)  24.2 us
    ppermute x12, starting transfers between devices, ring(): return lax.ppermute(a, 'x', [(i, (i + step) % 4) for i in range(4)])  18.7 us
    pallas_call x2, Pallas kernels, dispatch(): pl.pallas_call(functools.partial(dispatch_kernel, part=part), grid=(PEERS...  7.59 us
    unnamed x30, local copies, waits for them, and re-layouts  6.81 us
    ppermute x2, starting transfers between devices, swap(): return lax.ppermute(a, 'yh', [(0, 1), (1, 0)])  6.4 us
  transfers between devices with their start and end apart: 18, of which 9 were waited for; matrix products, arithmetic and copies ran while one was open for 3% of the time, Pallas kernels for 28%

commit v1 on v0

--- a/solution.py
+++ b/solution.py
@@ -10,8 +10,9 @@
 
 H = 8
 DS = 512
+CAP = 64
 PEERS = 32
-SLOTS = (40, 24)
+SLOTS = (32, 32)
 GROUP = 8
 SUBS = 1024
 EXTRA = 8
@@ -120,7 +121,7 @@
     weights = take(2 * pairs)
     before = take(1)[0] if part else None
     acc_in, router_in = (None, None) if begin else take(2)
-    router_first = take(1)[0] if last else None
+    router_first = take(2)[0] if last else None
     outs = take(2 * pairs if part else 1)
     (dx_out,) = take(1)
     router_out = None if last else take(1)[0]
@@ -199,7 +200,8 @@
             dbuf[:, :, g * DS : (g + 1) * DS] = rows[:, g * EXTRA : (g + 1) * EXTRA, :]
         if last:
             router_rows(dbuf, slots // EXTRA * DS, router_first[...], router)
-        save = pltpu.make_async_copy(dbuf, dx_out, asem)
+        here = pl.ds(part * SLOTS[0] // EXTRA * DS, dbuf.shape[2])
+        save = pltpu.make_async_copy(dbuf, dx_out.at[:, :, here], asem)
     else:
         save = pltpu.make_async_copy(acc, dx_out, asem)
     save.start()
@@ -229,14 +231,14 @@
         args += [in_hbm(carry[0]), carry[1]]
         in_specs += [HBM, WHOLE]
     if last:
-        args += [first]
-        in_specs += [WHOLE]
+        args += [first[1], in_hbm(first[0])]
+        in_specs += [WHOLE, HBM]
     if part:
         out_shape = [pltpu.HBM((3, SH, DS), BF)] * (2 * pairs)
     else:
         out_shape = [pltpu.HBM((3, pairs * UNITS, DS), F32)]
     if end:
-        out_shape += [pltpu.HBM((PEERS, EXTRA, width), BF)]
+        out_shape += [pltpu.HBM((PEERS, EXTRA, CAP // EXTRA * DS + 128), BF)]
     else:
         out_shape += [pltpu.HBM((rows, DS), F32)]
     out_specs = [HBM] * len(out_shape)
@@ -250,6 +252,7 @@
         in_specs=in_specs,
         out_specs=out_specs,
         out_shape=out_shape,
+        input_output_aliases={len(args) - 1: 2 * pairs} if last else {},
         scratch_shapes=[
             pltpu.VMEM((8, 128, 128) if part else (PEERS, 2 * slots, DS), BF),
             pltpu.VMEM((rows, DS), F32),
@@ -263,7 +266,7 @@
             pltpu.SemaphoreType.DMA((pairs,)),
             pltpu.SemaphoreType.DMA((pairs, 2)),
         ],
-        compiler_params=params(44),
+        compiler_params=params(36),
     )(*args)
 
 
@@ -282,32 +285,25 @@
 
 def slot_rows(back, part):
     slots = SLOTS[part]
-    groups = [back[:, :, g * DS : (g + 1) * DS] for g in range(slots // EXTRA)]
+    base = part * SLOTS[0] // EXTRA
+    groups = [
+        back[:, :, (base + g) * DS : (base + g + 1) * DS] for g in range(slots // EXTRA)
+    ]
     return jnp.concatenate(groups, axis=1).reshape(PEERS * slots, DS)
 
 
-def combine_first_kernel(table, back, out):
-    codes = columns(table)[0]
-    rows = slot_rows(back, 0)
-    count = 256
-    for b in range(SUBS // count):
-        out[b * count : (b + 1) * count, :] = contract(
-            picks(codes, 0, b * count, count), rows, 1, 0
-        )
-
-
-def combine_last_kernel(table, part, back, out, probs):
+def combine_kernel(table, back, out, probs):
     codes, weight, peer, slot = columns(table)
-    rows = slot_rows(back, 1)
+    rows = [slot_rows(back, part) for part in range(2)]
     count = 256
     n = count // 128
     for b in range(SUBS // count):
-        got = contract(picks(codes, 1, b * count, count), rows, 1, 0)
-        got = (got + part[b * count : (b + 1) * count, :]).astype(BF)
+        got = contract(picks(codes, 0, b * count, count), rows[0], 1, 0)
+        got = (got + contract(picks(codes, 1, b * count, count), rows[1], 1, 0)).astype(BF)
         for k in range(n):
             h = b * n + k
             out[:, h * DS : (h + 1) * DS] = got[k * 128 : (k + 1) * 128]
-    at = SLOTS[1] // EXTRA * DS
+    at = CAP // EXTRA * DS
     routers = back[:, :, at : at + 128].reshape(PEERS * EXTRA, 128)
     source = lax.broadcasted_iota(jnp.int32, (SUBS, PEERS * EXTRA), 1)
     lane = lax.broadcasted_iota(jnp.int32, (SUBS, 128), 1)
@@ -321,76 +317,50 @@
     probs[...] = jnp.transpose(both)[0:8, :]
 
 
-def combine_first(table, back):
+def combine(table, back):
     return pl.pallas_call(
-        combine_first_kernel,
-        out_shape=jax.ShapeDtypeStruct((SUBS, DS), F32),
-        compiler_params=params(),
-        name="combine_first",
-    )(table, in_hbm(back))
-
-
-def combine_last(table, part, back):
-    return pl.pallas_call(
-        combine_last_kernel,
+        combine_kernel,
         out_shape=[
             jax.ShapeDtypeStruct((SUBS // H, H * DS), BF),
             jax.ShapeDtypeStruct((8, SUBS), F32),
         ],
         compiler_params=params(),
-        name="combine_last",
-    )(table, part, back)
-
-
-def place(sources, grad_in, grad_out, at, sems):
-    copies = []
-    start = 0
-    for i, source in enumerate(sources):
-        here = pl.ds(start, source.shape[1])
-        start += source.shape[1]
-        copies += [
-            pltpu.make_async_copy(source.at[0:2], grad_in.at[at, :, here, :], sems.at[i, 0]),
-            pltpu.make_async_copy(source.at[2], grad_out.at[at, here, :], sems.at[i, 1]),
-        ]
-    for c in copies:
+        name="combine",
+    )(table, back)
+
+
+def final_kernel(which, own0, own1, own2, own3, other, grad_in, grad_out, total, sems):
+    a = which[0]
+
+    def copies(source, at, k):
+        return (
+            pltpu.make_async_copy(source.at[0:2], grad_in.at[at], sems.at[k, 0]),
+            pltpu.make_async_copy(source.at[2], grad_out.at[at], sems.at[k, 1]),
+        )
+
+    theirs = copies(other, 1 - a, 0)
+    for c in theirs:
         c.start()
-    for c in copies:
-        c.wait()
-
-
-def final_own_kernel(which, own0, own1, own2, own3, grad_in, grad_out, total, sems):
     for k in range(3):
         value = own0[k].astype(F32) + own1[k].astype(F32) + own2[k].astype(F32)
         total[k] = (value + own3[k].astype(F32)).astype(BF)
-    place([total], grad_in, grad_out, which[0], sems)
-
-
-def final_other_kernel(which, other, _in, _out, grad_in, grad_out, sems):
-    place([other], grad_in, grad_out, 1 - which[0], sems)
+    mine = copies(total, a, 1)
+    for c in mine:
+        c.start()
+    for c in theirs + mine:
+        c.wait()
 
 
 def final(which, own, other):
-    smem = pl.BlockSpec(memory_space=pltpu.SMEM)
-    out_shape = [pltpu.HBM((2, 2, SH, DS), BF), pltpu.HBM((2, SH, DS), BF)]
-    grads = pl.pallas_call(
-        final_own_kernel,
-        in_specs=[smem] + [WHOLE] * 4,
+    return pl.pallas_call(
+        final_kernel,
+        in_specs=[pl.BlockSpec(memory_space=pltpu.SMEM)] + [WHOLE] * 5,
         out_specs=[HBM, HBM],
-        out_shape=out_shape,
-        scratch_shapes=[pltpu.VMEM((3, SH, DS), BF), pltpu.SemaphoreType.DMA((1, 2))],
+        out_shape=[pltpu.HBM((2, 2, SH, DS), BF), pltpu.HBM((2, SH, DS), BF)],
+        scratch_shapes=[pltpu.VMEM((3, SH, DS), BF), pltpu.SemaphoreType.DMA((2, 2))],
         compiler_params=params(),
-        name="final_own",
-    )(which, *own)
-    return pl.pallas_call(
-        final_other_kernel,
-        in_specs=[smem, WHOLE, HBM, HBM],
-        out_specs=[HBM, HBM],
-        out_shape=out_shape,
-        input_output_aliases={2: 0, 3: 1},
-        scratch_shapes=[pltpu.SemaphoreType.DMA((1, 2))],
-        compiler_params=params(),
-        name="final_other",
-    )(which, other, *[in_hbm(g) for g in grads])
+        name="final",
+    )(which, *own, other)
 
 
 def ring(a, step):
@@ -412,8 +382,10 @@
 def layer(tokens, cotangent, expert_ids, slot_ids, route_probs, weights_in, weights_out):
     yh = lax.axis_index("yh")
     both = jnp.concatenate([weights_in, weights_out[:, None]], axis=1)
-    w_p = swap(jnp.where(yh == 0, both[1], both[0]))
-    w_o = jnp.where(yh == 0, both[0], both[1])
+    theirs = jnp.where(yh == 0, both[1], both[0])
+    w_p = swap(theirs)
+    mine = lax.optimization_barrier((both, theirs))[0]
+    w_o = jnp.where(yh == 0, mine[0], mine[1])
     w_o_m = ring(w_o, 1)
     w_o_p = ring(w_o, -1)
     w_p_m = ring(w_p, 1)
@@ -438,8 +410,7 @@
     far = [w_p_2, w_o_2]
     own = [w_p, w_o]
     dw_near, *carry = expert_part(0, z1, near)
-    dw_rest, back1, router1 = expert_part(0, z1, far + own, carry=carry, end=True)
-    back1 = exchange(back1)
+    dw_rest, *first = expert_part(0, z1, far + own, carry=carry, end=True)
     p_2, o_2, *carry = expert_part(1, z2, far, dw_rest, 0)
     p_2 = ring(p_2, 2)
     o_2 = ring(o_2, 2)
@@ -448,13 +419,12 @@
     p_m = ring(p_m, -1)
     o_p = ring(o_p, 1)
     o_m = ring(o_m, -1)
-    p_0, o_0, back2 = expert_part(1, z2, own, dw_rest, 1, carry, True, router1)
-    back2 = exchange(back2)
+    p_0, o_0, back = expert_part(1, z2, own, dw_rest, 1, carry, True, first)
+    back = exchange(back)
     other = swap(add(p_0, p_p, p_m, p_2))
     grad_in, grad_out = final(yh.astype(jnp.int32).reshape(1), (o_0, o_p, o_m, o_2), other)
 
-    part = combine_first(table, back1)
-    grad_tokens, probs = combine_last(table, part, back2)
+    grad_tokens, probs = combine(table, back)
     grad_probs = jnp.transpose(probs[0:2].reshape(2, H, SUBS // H), (2, 1, 0))
     return grad_tokens, grad_probs, grad_in, grad_out
 

time: 231 us -> 236 us (1.022)
  waiting for transfers between devices: 88.9 us -> 99.9 us
  other arithmetic: 7.05 us -> 3.08 us
  Pallas kernels: 69.7 us -> 66.8 us
  starting transfers between devices: 56.1 us -> 59 us
    ppermute x12, waiting for transfers between devices: 61.8 us -> 80.3 us  [ring(): return lax.ppermute(a, 'x', [(i, (i + step) % 4) for i in range(4)])]
    all_to_all x4 -> x3, starting transfers between devices: 31 us -> 35.8 us  [exchange(): return lax.all_to_all(a, PLANE, 0, 0, tiled=True)]
    all_to_all x4 -> x3, waiting for transfers between devices: 24.2 us -> 19.7 us  [exchange(): return lax.all_to_all(a, PLANE, 0, 0, tiled=True)]
    ppermute x2, waiting for transfers between devices: 2.95 us -> 0.01 us  [swap(): return lax.ppermute(a, 'yh', [(0, 1), (1, 0)])]
    pallas_call x4 -> x2, Pallas kernels: 8.75 us -> 6.1 us  [the longest x1 4.88 us: combine(): pl.pallas_call(combine_kernel, out_shape=[jax.ShapeDtypeStruct((SUBS // H...]
    ppermute x12, starting transfers between devices: 18.7 us -> 16.3 us  [ring(): return lax.ppermute(a, 'x', [(i, (i + step) % 4) for i in range(4)])]
    convert_element_type x1, other arithmetic: 2.8 us -> 0.38 us  [add(): return sum((a.astype(F32) for a in arrays)).astype(BF)]
  transfers between devices with their start and end apart: 18 -> 17, of which waited for: 9 -> 6; matrix products, arithmetic and copies ran while one was open for 3% -> 1% of each run, Pallas kernels for 28% -> 13%
where the time goes in v1:
time: 236 us
  waiting for transfers between devices  99.9 us (42%)
  Pallas kernels  66.8 us (28%)
  starting transfers between devices  59 us (25%)
  local copies, waits for them, and re-layouts  5.85 us (2%)
  other arithmetic  3.08 us (1%)
    ppermute x12, waiting for transfers between devices, ring(): return lax.ppermute(a, 'x', [(i, (i + step) % 4) for i in range(4)])  80.3 us
    pallas_call x5, Pallas kernels, expert_part(): pl.pallas_call(functools.partial(expert_kernel, part=part, pairs=pairs, f...  53.1 us
    all_to_all x3, starting transfers between devices, exchange(): return lax.all_to_all(a, PLANE, 0, 0, tiled=True)  35.8 us
    all_to_all x3, waiting for transfers between devices, exchange(): return lax.all_to_all(a, PLANE, 0, 0, tiled=True)  19.7 us
    ppermute x12, starting transfers between devices, ring(): return lax.ppermute(a, 'x', [(i, (i + step) % 4) for i in range(4)])  16.3 us
    pallas_call x2, Pallas kernels, dispatch(): pl.pallas_call(functools.partial(dispatch_kernel, part=part), grid=(PEERS...  7.68 us
    ppermute x2, starting transfers between devices, swap(): return lax.ppermute(a, 'yh', [(0, 1), (1, 0)])  6.87 us
    unnamed x30, local copies, waits for them, and re-layouts  5.23 us
  transfers between devices with their start and end apart: 17, of which 6 were waited for; matrix products, arithmetic and copies ran while one was open for 1% of the time, Pallas kernels for 13%

profile of v1, /device:TPU:0, one launch (start us, length us, event | category | flops | bytes accessed | tf_op | source)
XLA Modules:
  0.0 235.6 jit_solution(18296950370931455568)
XLA Ops:
  0.6 0.7 convert_element_type.28
  1.3 0.8 fusion.4
  2.2 0.0 copy-start
  2.2 1.2 copy-done
  3.4 1.2 copy-done.2
  4.6 3.8 %shard_map.103 = bf16[32,64,512]{2,1,0:T(8,128)(2,1)} custom-call(f32[8,1024]{1,0:T(8,128)S(1)} %maximum_bitcast_fusion.table, bf16[128,4096]{1,0:T(8,128)(2,1)S(1)} %copy-done, bf16[128,4096]{1,0:T(8,128)(2,1)S(1)} %copy-done.2), custom_call_target="tpu_custom_call" | custom-call | tf_op jit(solution)/shard_map/pallas_call | solution.py:60
  8.5 8.7 %all-to-all-start.1 = ((bf16[32,64,512]{2,1,0:T(8,128)(2,1)}), bf16[32,64,512]{2,1,0:T(8,128)(2,1)}, u32[]{:S(2)}, u32[]{:S(2)}) async-start(bf16[32,64,512]{2,1,0:T(8,128)(2,1)} %shard_map.103), calls=%async_computation.1 | async-start | bytes 4194304 | tf_op jit(solution)/shard_map/all_to_all | solution.py:375
  17.2 0.0 copy-start.1
  17.2 1.0 fusion.2
  18.2 3.2 %collective-permute-start = (bf16[3,224,512]{2,1,0:T(8,128)(2,1)}, bf16[3,224,512]{2,1,0:T(8,128)(2,1)}, u32[]{:S(2)}, u32[]{:S(2)}) collective-permute-start(bf16[3,224,512]{2,1,0:T(8,128)(2,1)} %fusion.2), channel_id=1, source_target_pairs={{0,16},{16,0},{1,17},{17,1},{2,18},{18,2},{3,19},{19,3},{4,20},{20... | collective-permute-start | bytes 2064392 | tf_op jit(solution)/shard_map/ppermute | solution.py:371
  21.4 3.8 %shard_map.102 = bf16[32,64,512]{2,1,0:T(8,128)(2,1)} custom-call(f32[8,1024]{1,0:T(8,128)S(1)} %maximum_bitcast_fusion.table, bf16[128,4096]{1,0:T(8,128)(2,1)S(1)} %copy-done.1, bf16[128,4096]{1,0:T(8,128)(2,1)S(1)} %copy-done.3), custom_call_target="tpu_custom_call" | custom-call | tf_op jit(solution)/shard_map/pallas_call | solution.py:60
  25.3 19.7 %all-to-all-done.1.refs_0_ = bf16[32,64,512]{2,1,0:T(8,128)(2,1)} async-done(((bf16[32,64,512]{2,1,0:T(8,128)(2,1)}), bf16[32,64,512]{2,1,0:T(8,128)(2,1)}, u32[]{:S(2)}, u32[]{:S(2)}) %all-to-all-start.1) | async-done | bytes 2097184 | tf_op jit(solution)/shard_map/all_to_all | solution.py:375
  44.9 19.6 %all-to-all-start = ((bf16[32,64,512]{2,1,0:T(8,128)(2,1)}), bf16[32,64,512]{2,1,0:T(8,128)(2,1)S(1)}, u32[]{:S(2)}, u32[]{:S(2)}) async-start(bf16[32,64,512]{2,1,0:T(8,128)(2,1)} %shard_map.102), calls=%async_computation | async-start | bytes 4194304 | tf_op jit(solution)/shard_map/all_to_all | solution.py:375
  64.5 0.1 pad_maximum_fusion
  64.6 0.1 select_bitcast_fusion.refs_4_.refs_2_
  64.7 0.0 copy-start.5
  64.7 2.8 %collective-permute-start.3 = (bf16[3,224,512]{2,1,0:T(8,128)(2,1)S(1)}, bf16[3,224,512]{2,1,0:T(8,128)(2,1)S(1)}, u32[]{:S(2)}, u32[]{:S(2)}) collective-permute-start(bf16[3,224,512]{2,1,0:T(8,128)(2,1)S(1)} %select_bitcast_fusion.refs_4_.refs_2_), channel_id=1, source_target_pairs={{0,96},{32,0},{64,32},{96,64},{1,97},{33,1},{65,33},{97,65},{2,98}... | collective-permute-start | bytes 2064392 | tf_op jit(solution)/shard_map/ppermute | solution.py:367
  67.6 0.0 collective-permute-done.refs_3_.refs_1_
  67.6 0.0 collective-permute-start.1
  67.6 0.8 collective-permute-start.6
  68.3 2.5 %collective-permute-start.5 = (bf16[3,224,512]{2,1,0:T(8,128)(2,1)}, bf16[3,224,512]{2,1,0:T(8,128)(2,1)S(1)}, u32[]{:S(2)}, u32[]{:S(2)}) collective-permute-start(bf16[3,224,512]{2,1,0:T(8,128)(2,1)} %collective-permute-done.refs_3_.refs_1_), channel_id=1, source_target_pairs={{0,96},{32,0},{64,32},{96,64},{1,97},{33,1},{65,33},{97,65},{2,98}... | collective-permute-start | bytes 2064392 | tf_op jit(solution)/shard_map/ppermute | solution.py:367
  70.8 12.6 %collective-permute-done.3.refs_3_ = bf16[3,224,512]{2,1,0:T(8,128)(2,1)S(1)} collective-permute-done((bf16[3,224,512]{2,1,0:T(8,128)(2,1)S(1)}, bf16[3,224,512]{2,1,0:T(8,128)(2,1)S(1)}, u32[]{:S(2)}, u32[]{:S(2)}) %collective-permute-start.3) | collective-permute-done | bytes 688160 | tf_op jit(solution)/shard_map/ppermute | solution.py:367
  83.4 3.7 %collective-permute-start.4 = (bf16[3,224,512]{2,1,0:T(8,128)(2,1)S(1)}, bf16[3,224,512]{2,1,0:T(8,128)(2,1)S(1)}, u32[]{:S(2)}, u32[]{:S(2)}) collective-permute-start(bf16[3,224,512]{2,1,0:T(8,128)(2,1)S(1)} %collective-permute-done.3.refs_3_), channel_id=1, source_target_pairs={{0,96},{32,0},{64,32},{96,64},{1,97},{33,1},{65,33},{97,65},{2,98}... | collective-permute-start | bytes 2064392 | tf_op jit(solution)/shard_map/ppermute | solution.py:367
  87.1 0.2 collective-permute-done.1.refs_2_
  87.3 0.0 collective-permute-start.2
  87.3 14.7 %collective-permute-done.6.refs_4_ = bf16[3,224,512]{2,1,0:T(8,128)(2,1)S(1)} collective-permute-done((bf16[3,224,512]{2,1,0:T(8,128)(2,1)S(1)}, bf16[3,224,512]{2,1,0:T(8,128)(2,1)S(1)}, u32[]{:S(2)}, u32[]{:S(2)}) %collective-permute-start.6) | collective-permute-done | bytes 688160 | tf_op jit(solution)/shard_map/ppermute | solution.py:367
  102.1 0.9 copy-done.9
  102.9 0.8 copy-done.10
  103.8 12.4 %shard_map.104 = (f32[3,896,512]{2,1,0:T(8,128)}, f32[1024,512]{1,0:T(8,128)}, f32[8,1024]{1,0:T(8,128)S(1)}) custom-call(bf16[32,64,512]{2,1,0:T(8,128)(2,1)} %all-to-all-done.1.refs_0_, bf16[3,224,512]{2,1,0:T(8,128)(2,1)} %copy-done.10, bf16[3,224,512]{2,1,0:T(8,128)(2,1)} %copy-done.8, bf16[3,224,512]{2,1,0:T(8,128)(2,1)} %copy-done.7, ...), custom_call_target="tpu_custom_call" | custom-call | tf_op jit(solution)/shard_map/pallas_call | solution.py:248
  116.2 0.0 copy-start.12
  116.3 0.8 copy-done.11
  117.1 0.2 copy-done.12
  117.3 12.7 %shard_map.105 = (f32[3,896,512]{2,1,0:T(8,128)}, bf16[32,8,4224]{2,1,0:T(8,128)(2,1)}, f32[8,1024]{1,0:T(8,128)S(1)}) custom-call(bf16[32,64,512]{2,1,0:T(8,128)(2,1)} %all-to-all-done.1.refs_0_, bf16[3,224,512]{2,1,0:T(8,128)(2,1)} %copy-done.12, bf16[3,224,512]{2,1,0:T(8,128)(2,1)} %copy-done.11, ...), custom_call_target="tpu_custom_call" | custom-call | tf_op jit(solution)/shard_map/pallas_call | solution.py:248
  130.0 7.8 %shard_map.106 = (bf16[3,224,512]{2,1,0:T(8,128)(2,1)}, bf16[3,224,512]{2,1,0:T(8,128)(2,1)}, f32[1024,512]{1,0:T(8,128)}, f32[8,1024]{1,0:T(8,128)S(1)}) custom-call(bf16[32,64,512]{2,1,0:T(8,128)(2,1)S(1)} %all-to-all-done.refs_0_, bf16[3,224,512]{2,1,0:T(8,128)(2,1)} %copy-done.12, bf16[3,224,512]{2,1,0:T(8,128)(2,1)} %copy-done.11, ...), custom_call_target="tpu_custom_call" | custom-call | tf_op jit(solution)/shard_map/pallas_call | solution.py:248
  137.8 12.6 %shard_map.107 = (bf16[3,224,512]{2,1,0:T(8,128)(2,1)}, bf16[3,224,512]{2,1,0:T(8,128)(2,1)}, bf16[3,224,512]{2,1,0:T(8,128)(2,1)}, bf16[3,224,512]{2,1,0:T(8,12...) custom-call(bf16[32,64,512]{2,1,0:T(8,128)(2,1)S(1)} %all-to-all-done.refs_0_, bf16[3,224,512]{2,1,0:T(8,128)(2,1)} %copy-done.10, ...), custom_call_target="tpu_custom_call" | custom-call | tf_op jit(solution)/shard_map/pallas_call | solution.py:248
  150.4 7.6 %shard_map.108 = (bf16[3,224,512]{2,1,0:T(8,128)(2,1)}, bf16[3,224,512]{2,1,0:T(8,128)(2,1)}, bf16[32,8,4224]{2,1,0:T(8,128)(2,1)}) custom-call(bf16[32,64,512]{2,1,0:T(8,128)(2,1)S(1)} %all-to-all-done.refs_0_, bf16[3,224,512]{2,1,0:T(8,128)(2,1)} %collective-permute-done.refs_3_.refs_1_, ...), custom_call_target="tpu_custom_call", output_to_operand_aliasing={{2}: (7, {})} | custom-call | tf_op jit(solution)/shard_map/pallas_call | solution.py:248
  158.0 7.6 %all-to-all-start.2 = ((bf16[32,8,4224]{2,1,0:T(8,128)(2,1)}), bf16[32,8,4224]{2,1,0:T(8,128)(2,1)S(1)}, u32[]{:S(2)}, u32[]{:S(2)}) async-start(bf16[32,8,4224]{2,1,0:T(8,128)(2,1)} %get-tuple-element.39), calls=%async_computation.2 | async-start | bytes 4325376 | tf_op jit(solution)/shard_map/all_to_all | solution.py:375
  165.5 0.1 collective-permute-start.10
  165.6 3.2 %collective-permute-start.11 = (bf16[3,224,512]{2,1,0:T(8,128)(2,1)}, bf16[3,224,512]{2,1,0:T(8,128)(2,1)S(1)}, u32[]{:S(2)}, u32[]{:S(2)}) collective-permute-start(bf16[3,224,512]{2,1,0:T(8,128)(2,1)} %get-tuple-element.48), channel_id=1, source_target_pairs={{0,96},{32,0},{64,32},{96,64},{1,97},{33,1},{65,33},{97,65},{2,98}... | collective-permute-start | bytes 2064392 | tf_op jit(solution)/shard_map/ppermute | solution.py:367
  168.9 0.9 collective-permute-start.7
  169.7 2.4 %collective-permute-start.8 = (bf16[3,224,512]{2,1,0:T(8,128)(2,1)}, bf16[3,224,512]{2,1,0:T(8,128)(2,1)S(1)}, u32[]{:S(2)}, u32[]{:S(2)}) collective-permute-start(bf16[3,224,512]{2,1,0:T(8,128)(2,1)} %get-tuple-element.44), channel_id=1, source_target_pairs={{0,96},{32,0},{64,32},{96,64},{1,97},{33,1},{65,33},{97,65},{2,98}... | collective-permute-start | bytes 2064392 | tf_op jit(solution)/shard_map/ppermute | solution.py:367
  172.1 28.0 %collective-permute-done.10 = bf16[3,224,512]{2,1,0:T(8,128)(2,1)S(1)} collective-permute-done((bf16[3,224,512]{2,1,0:T(8,128)(2,1)}, bf16[3,224,512]{2,1,0:T(8,128)(2,1)S(1)}, u32[]{:S(2)}, u32[]{:S(2)}) %collective-permute-start.10) | collective-permute-done | bytes 688160 | tf_op jit(solution)/shard_map/ppermute | solution.py:367
  200.1 0.4 add_convert_fusion
  200.5 3.6 %collective-permute-start.13 = (bf16[3,224,512]{2,1,0:T(8,128)(2,1)S(1)}, bf16[3,224,512]{2,1,0:T(8,128)(2,1)S(1)}, u32[]{:S(2)}, u32[]{:S(2)}) collective-permute-start(bf16[3,224,512]{2,1,0:T(8,128)(2,1)S(1)} %add_convert_fusion), channel_id=1, source_target_pairs={{0,16},{16,0},{1,17},{17,1},{2,18},{18,2},{3,19},{19,3},{4,20},{20... | collective-permute-start | bytes 2064392 | tf_op jit(solution)/shard_map/ppermute | solution.py:371
  204.1 24.7 %collective-permute-done.7.own1 = bf16[3,224,512]{2,1,0:T(8,128)(2,1)S(1)} collective-permute-done((bf16[3,224,512]{2,1,0:T(8,128)(2,1)}, bf16[3,224,512]{2,1,0:T(8,128)(2,1)S(1)}, u32[]{:S(2)}, u32[]{:S(2)}) %collective-permute-start.7) | collective-permute-done | bytes 688160 | tf_op jit(solution)/shard_map/ppermute | solution.py:367
  228.9 1.2 final.1
  230.1 4.9 %combine.1 = (bf16[128,4096]{1,0:T(8,128)(2,1)}, f32[8,1024]{1,0:T(8,128)S(1)}) custom-call(f32[8,1024]{1,0:T(8,128)S(1)} %maximum_bitcast_fusion.table, bf16[32,8,4224]{2,1,0:T(8,128)(2,1)S(1)} %all-to-all-done.2.back), custom_call_target="tpu_custom_call" | custom-call | tf_op jit(solution)/shard_map/combine/pallas_call | solution.py:321
  235.0 0.6 slice_bitcast_fusion
  (34 shorter events, 0.1 us)
Async XLA Ops:
  2.2 1.2 copy-start
  3.4 1.2 copy-start.2
  8.5 8.8 %copy-start.6 = (bf16[2,2,224,512]{3,2,1,0:T(8,128)(2,1)S(1)}, bf16[2,2,224,512]{3,2,1,0:T(8,128)(2,1)}, u32[]{:S(2)}) copy-start(bf16[2,2,224,512]{3,2,1,0:T(8,128)(2,1)} %param.12) | copy-start | bytes 2752516
  8.5 8.8 %copy-start.13 = (bf16[2,224,512]{2,1,0:T(8,128)(2,1)S(1)}, bf16[2,224,512]{2,1,0:T(8,128)(2,1)}, u32[]{:S(2)}) copy-start(bf16[2,224,512]{2,1,0:T(8,128)(2,1)} %param.13) | copy-start | bytes 1376260
  8.5 13.0 %copy-start.3 = (bf16[128,4096]{1,0:T(8,128)(2,1)S(1)}, bf16[128,4096]{1,0:T(8,128)(2,1)}, u32[]{:S(2)}) copy-start(bf16[128,4096]{1,0:T(8,128)(2,1)} %cot.3) | copy-start | bytes 3145732
  8.5 36.5 %all-to-all-start.1 = ((bf16[32,64,512]{2,1,0:T(8,128)(2,1)}), bf16[32,64,512]{2,1,0:T(8,128)(2,1)}, u32[]{:S(2)}, u32[]{:S(2)}) async-start(bf16[32,64,512]{2,1,0:T(8,128)(2,1)} %shard_map.103), calls=%async_computation.1 | async-start | bytes 4194304 | tf_op jit(solution)/shard_map/all_to_all | solution.py:375
  17.2 4.2 %copy-start.1 = (bf16[128,4096]{1,0:T(8,128)(2,1)S(1)}, bf16[128,4096]{1,0:T(8,128)(2,1)}, u32[]{:S(2)}) copy-start(bf16[128,4096]{1,0:T(8,128)(2,1)} %tok.3) | copy-start | bytes 3145732
  18.2 49.4 %collective-permute-start = (bf16[3,224,512]{2,1,0:T(8,128)(2,1)}, bf16[3,224,512]{2,1,0:T(8,128)(2,1)}, u32[]{:S(2)}, u32[]{:S(2)}) collective-permute-start(bf16[3,224,512]{2,1,0:T(8,128)(2,1)} %fusion.2), channel_id=1, source_target_pairs={{0,16},{16,0},{1,17},{17,1},{2,18},{18,2},{3,19},{19,3},{4,20},{20... | collective-permute-start | bytes 2064392 | tf_op jit(solution)/shard_map/ppermute | solution.py:371
  44.9 85.1 %all-to-all-start = ((bf16[32,64,512]{2,1,0:T(8,128)(2,1)}), bf16[32,64,512]{2,1,0:T(8,128)(2,1)S(1)}, u32[]{:S(2)}, u32[]{:S(2)}) async-start(bf16[32,64,512]{2,1,0:T(8,128)(2,1)} %shard_map.102), calls=%async_computation | async-start | bytes 4194304 | tf_op jit(solution)/shard_map/all_to_all | solution.py:375
  64.7 51.5 %copy-start.5 = (bf16[3,224,512]{2,1,0:T(8,128)(2,1)}, bf16[3,224,512]{2,1,0:T(8,128)(2,1)S(1)}, u32[]{:S(2)}) copy-start(bf16[3,224,512]{2,1,0:T(8,128)(2,1)S(1)} %select_bitcast_fusion.refs_4_.refs_2_) | copy-start | bytes 2064388
  64.7 18.7 %collective-permute-start.3 = (bf16[3,224,512]{2,1,0:T(8,128)(2,1)S(1)}, bf16[3,224,512]{2,1,0:T(8,128)(2,1)S(1)}, u32[]{:S(2)}, u32[]{:S(2)}) collective-permute-start(bf16[3,224,512]{2,1,0:T(8,128)(2,1)S(1)} %select_bitcast_fusion.refs_4_.refs_2_), channel_id=1, source_target_pairs={{0,96},{32,0},{64,32},{96,64},{1,97},{33,1},{65,33},{97,65},{2,98}... | collective-permute-start | bytes 2064392 | tf_op jit(solution)/shard_map/ppermute | solution.py:367
  67.6 19.7 %collective-permute-start.1 = (bf16[3,224,512]{2,1,0:T(8,128)(2,1)}, bf16[3,224,512]{2,1,0:T(8,128)(2,1)S(1)}, u32[]{:S(2)}, u32[]{:S(2)}) collective-permute-start(bf16[3,224,512]{2,1,0:T(8,128)(2,1)} %collective-permute-done.refs_3_.refs_1_), channel_id=1, source_target_pairs={{0,32},{32,64},{64,96},{96,0},{1,33},{33,65},{65,97},{97,1},{2,34}... | collective-permute-start | bytes 2064392 | tf_op jit(solution)/shard_map/ppermute | solution.py:367
  67.6 34.5 %collective-permute-start.6 = (bf16[3,224,512]{2,1,0:T(8,128)(2,1)S(1)}, bf16[3,224,512]{2,1,0:T(8,128)(2,1)S(1)}, u32[]{:S(2)}, u32[]{:S(2)}) collective-permute-start(bf16[3,224,512]{2,1,0:T(8,128)(2,1)S(1)} %select_bitcast_fusion.refs_4_.refs_2_), channel_id=1, source_target_pairs={{0,32},{32,64},{64,96},{96,0},{1,33},{33,65},{65,97},{97,1},{2,34}... | collective-permute-start | bytes 2064392 | tf_op jit(solution)/shard_map/ppermute | solution.py:367
  68.3 33.7 %collective-permute-start.5 = (bf16[3,224,512]{2,1,0:T(8,128)(2,1)}, bf16[3,224,512]{2,1,0:T(8,128)(2,1)S(1)}, u32[]{:S(2)}, u32[]{:S(2)}) collective-permute-start(bf16[3,224,512]{2,1,0:T(8,128)(2,1)} %collective-permute-done.refs_3_.refs_1_), channel_id=1, source_target_pairs={{0,96},{32,0},{64,32},{96,64},{1,97},{33,1},{65,33},{97,65},{2,98}... | collective-permute-start | bytes 2064392 | tf_op jit(solution)/shard_map/ppermute | solution.py:367
  83.4 18.7 %copy-start.7 = (bf16[3,224,512]{2,1,0:T(8,128)(2,1)}, bf16[3,224,512]{2,1,0:T(8,128)(2,1)S(1)}, u32[]{:S(2)}) copy-start(bf16[3,224,512]{2,1,0:T(8,128)(2,1)S(1)} %collective-permute-done.3.refs_3_) | copy-start | bytes 2064388
  83.4 32.8 %collective-permute-start.4 = (bf16[3,224,512]{2,1,0:T(8,128)(2,1)S(1)}, bf16[3,224,512]{2,1,0:T(8,128)(2,1)S(1)}, u32[]{:S(2)}, u32[]{:S(2)}) collective-permute-start(bf16[3,224,512]{2,1,0:T(8,128)(2,1)S(1)} %collective-permute-done.3.refs_3_), channel_id=1, source_target_pairs={{0,96},{32,0},{64,32},{96,64},{1,97},{33,1},{65,33},{97,65},{2,98}... | collective-permute-start | bytes 2064392 | tf_op jit(solution)/shard_map/ppermute | solution.py:367
  87.3 14.8 %copy-start.8 = (bf16[3,224,512]{2,1,0:T(8,128)(2,1)}, bf16[3,224,512]{2,1,0:T(8,128)(2,1)S(1)}, u32[]{:S(2)}) copy-start(bf16[3,224,512]{2,1,0:T(8,128)(2,1)S(1)} %collective-permute-done.1.refs_2_) | copy-start | bytes 2064388
  87.3 28.9 %collective-permute-start.2 = (bf16[3,224,512]{2,1,0:T(8,128)(2,1)S(1)}, bf16[3,224,512]{2,1,0:T(8,128)(2,1)S(1)}, u32[]{:S(2)}, u32[]{:S(2)}) collective-permute-start(bf16[3,224,512]{2,1,0:T(8,128)(2,1)S(1)} %collective-permute-done.1.refs_2_), channel_id=1, source_target_pairs={{0,32},{32,64},{64,96},{96,0},{1,33},{33,65},{65,97},{97,1},{2,34}... | collective-permute-start | bytes 2064392 | tf_op jit(solution)/shard_map/ppermute | solution.py:367
  102.0 0.9 copy-start.9
  102.9 0.8 copy-start.10
  116.2 0.9 copy-start.11
  116.2 1.1 copy-start.12
  158.0 42.1 %copy-start.14 = (bf16[3,224,512]{2,1,0:T(8,128)(2,1)S(1)}, bf16[3,224,512]{2,1,0:T(8,128)(2,1)}, u32[]{:S(2)}) copy-start(bf16[3,224,512]{2,1,0:T(8,128)(2,1)} %get-tuple-element.46) | copy-start | bytes 2064388
  158.0 72.2 %all-to-all-start.2 = ((bf16[32,8,4224]{2,1,0:T(8,128)(2,1)}), bf16[32,8,4224]{2,1,0:T(8,128)(2,1)S(1)}, u32[]{:S(2)}, u32[]{:S(2)}) async-start(bf16[32,8,4224]{2,1,0:T(8,128)(2,1)} %get-tuple-element.39), calls=%async_computation.2 | async-start | bytes 4325376 | tf_op jit(solution)/shard_map/all_to_all | solution.py:375
  165.5 34.5 %collective-permute-start.10 = (bf16[3,224,512]{2,1,0:T(8,128)(2,1)}, bf16[3,224,512]{2,1,0:T(8,128)(2,1)S(1)}, u32[]{:S(2)}, u32[]{:S(2)}) collective-permute-start(bf16[3,224,512]{2,1,0:T(8,128)(2,1)} %get-tuple-element.47), channel_id=1, source_target_pairs={{0,32},{32,64},{64,96},{96,0},{1,33},{33,65},{65,97},{97,1},{2,34}... | collective-permute-start | bytes 2064392 | tf_op jit(solution)/shard_map/ppermute | solution.py:367
  165.6 34.5 %collective-permute-start.11 = (bf16[3,224,512]{2,1,0:T(8,128)(2,1)}, bf16[3,224,512]{2,1,0:T(8,128)(2,1)S(1)}, u32[]{:S(2)}, u32[]{:S(2)}) collective-permute-start(bf16[3,224,512]{2,1,0:T(8,128)(2,1)} %get-tuple-element.48), channel_id=1, source_target_pairs={{0,96},{32,0},{64,32},{96,64},{1,97},{33,1},{65,33},{97,65},{2,98}... | collective-permute-start | bytes 2064392 | tf_op jit(solution)/shard_map/ppermute | solution.py:367
  168.8 31.2 %collective-permute-start.12 = (bf16[3,224,512]{2,1,0:T(8,128)(2,1)}, bf16[3,224,512]{2,1,0:T(8,128)(2,1)S(1)}, u32[]{:S(2)}, u32[]{:S(2)}) collective-permute-start(bf16[3,224,512]{2,1,0:T(8,128)(2,1)} %get-tuple-element.49), channel_id=1, source_target_pairs={{0,64},{32,96},{64,0},{96,32},{1,65},{33,97},{65,1},{97,33},{2,66}... | collective-permute-start | bytes 2064392 | tf_op jit(solution)/shard_map/ppermute | solution.py:367
  168.9 60.0 %collective-permute-start.7 = (bf16[3,224,512]{2,1,0:T(8,128)(2,1)}, bf16[3,224,512]{2,1,0:T(8,128)(2,1)S(1)}, u32[]{:S(2)}, u32[]{:S(2)}) collective-permute-start(bf16[3,224,512]{2,1,0:T(8,128)(2,1)} %get-tuple-element.43), channel_id=1, source_target_pairs={{0,32},{32,64},{64,96},{96,0},{1,33},{33,65},{65,97},{97,1},{2,34}... | collective-permute-start | bytes 2064392 | tf_op jit(solution)/shard_map/ppermute | solution.py:367
  169.7 59.2 %collective-permute-start.8 = (bf16[3,224,512]{2,1,0:T(8,128)(2,1)}, bf16[3,224,512]{2,1,0:T(8,128)(2,1)S(1)}, u32[]{:S(2)}, u32[]{:S(2)}) collective-permute-start(bf16[3,224,512]{2,1,0:T(8,128)(2,1)} %get-tuple-element.44), channel_id=1, source_target_pairs={{0,96},{32,0},{64,32},{96,64},{1,97},{33,1},{65,33},{97,65},{2,98}... | collective-permute-start | bytes 2064392 | tf_op jit(solution)/shard_map/ppermute | solution.py:367
  200.1 28.8 %collective-permute-start.9 = (bf16[3,224,512]{2,1,0:T(8,128)(2,1)}, bf16[3,224,512]{2,1,0:T(8,128)(2,1)S(1)}, u32[]{:S(2)}, u32[]{:S(2)}) collective-permute-start(bf16[3,224,512]{2,1,0:T(8,128)(2,1)} %get-tuple-element.45), channel_id=1, source_target_pairs={{0,64},{32,96},{64,0},{96,32},{1,65},{33,97},{65,1},{97,33},{2,66}... | collective-permute-start | bytes 2064392 | tf_op jit(solution)/shard_map/ppermute | solution.py:367
  200.1 28.8 %copy-start.4 = (bf16[3,224,512]{2,1,0:T(8,128)(2,1)S(1)}, bf16[3,224,512]{2,1,0:T(8,128)(2,1)}, u32[]{:S(2)}) copy-start(bf16[3,224,512]{2,1,0:T(8,128)(2,1)} %get-tuple-element.42.own0) | copy-start | bytes 2064388
  200.5 28.4 %collective-permute-start.13 = (bf16[3,224,512]{2,1,0:T(8,128)(2,1)S(1)}, bf16[3,224,512]{2,1,0:T(8,128)(2,1)S(1)}, u32[]{:S(2)}, u32[]{:S(2)}) collective-permute-start(bf16[3,224,512]{2,1,0:T(8,128)(2,1)S(1)} %add_convert_fusion), channel_id=1, source_target_pairs={{0,16},{16,0},{1,17},{17,1},{2,18},{18,2},{3,19},{19,3},{4,20},{20... | collective-permute-start | bytes 2064392 | tf_op jit(solution)/shard_map/ppermute | solution.py:371
